TPU v7x, 32 devices: a whole 2x2x4 slice. The times are simulated.
32 devices in a mesh: section: 4 (over x, core), tp: 8 (over z, y).
Axes of the slice: x: 2, y: 2, z: 4, core: 2. Of those that a mesh axis runs over, the one named last changes fastest.
Arguments:
- pending_activation: bfloat16 [4, 128, 4096], P('section'), may hold values from -6 to 6
- admissible_microbatches: bfloat16 [4, 128, 4096], P(None, None, 'tp'), may hold values from -6 to 6
- arrival_plan: int32 [4], replicated, may hold values from 0 to 3, each once
- vanished_hop: int32 [1], replicated, may hold values from 1 to 3
- query_key_value_matrices: bfloat16 [4, 4096, 3, 2048], P('section', None, None, 'tp')
- mixing_projection_matrices: bfloat16 [4, 2048, 4096], P('section', 'tp'), may hold values from -0.125 to 0.125
- normalizer_factors: bfloat16 [4, 4096], P('section'), may hold values from 0.25 to 1.75
Outputs:
- activation_later: bfloat16 [4, 128, 4096], P('section')
- standby_input: bfloat16 [4, 128, 4096], P('section', None, 'tp')
Inputs may be any that keep to these rules, and one draw needn't show every extreme that they name: `vanished_hop`: the preempted section is not the first. `arrival_plan`: each micro-batch index once.
All inputs are finite; a program needn't handle non-finite values.
Results may differ from a plain program's by a relative error of at most 0.013.
Values may be sent and summed in bfloat16 or wider, within the bound.
A program may use at most 64 MiB of HBM per device.

v0:
```python
import jax
import jax.numpy as jnp
from jax import lax
from jax.sharding import PartitionSpec as P

HD = 128
TICKS = 3


NORM_EPS = 1e-05


def shifted(value, axis, steps):
    count = lax.axis_size(axis)
    pairs = [(source, (source + steps) % count) for source in range(count)]
    return lax.ppermute(value, axis, pairs)


def layer_norm(x_rows, scale_row):
    widened = x_rows.astype(jnp.float32)
    row_mean = jnp.mean(widened, axis=-1, keepdims=True)
    centered = widened - row_mean
    row_var = jnp.mean(centered * centered, axis=-1, keepdims=True)
    return (centered * lax.rsqrt(row_var + NORM_EPS) * scale_row.astype(jnp.float32)).astype(
        jnp.bfloat16
    )


def attend(normed, w_in, w_out):
    row_count = normed.shape[0]
    col_count = w_in.shape[2]
    head_count = col_count // HD
    projected = jnp.dot(
        normed, w_in.reshape(w_in.shape[0], 3 * col_count), preferred_element_type=jnp.float32
    )
    projected = projected.astype(jnp.bfloat16).reshape(row_count, 3, head_count, HD)
    queries = projected[:, 0]
    key_rows = projected[:, 1]
    values = projected[:, 2]
    scores = jnp.einsum(
        "qhd,khd->hqk", queries, key_rows, preferred_element_type=jnp.float32
    ) * HD ** (-0.5)
    causal = jnp.arange(row_count)[:, None] >= jnp.arange(row_count)[None, :]
    scores = jnp.where(causal[None], scores, -jnp.inf)
    row_max = jnp.max(scores, axis=-1, keepdims=True)
    weights = jnp.exp(scores - row_max)
    probs = (weights / jnp.sum(weights, axis=-1, keepdims=True)).astype(jnp.bfloat16)
    context = jnp.einsum("hqk,khd->qhd", probs, values, preferred_element_type=jnp.float32)
    context = context.astype(jnp.bfloat16).reshape(row_count, col_count)
    return jnp.dot(context, w_out, preferred_element_type=jnp.float32)


def per_device(
    pending_activation,
    admissible_microbatches,
    arrival_plan,
    vanished_hop,
    query_key_value_matrices,
    mixing_projection_matrices,
    normalizer_factors,
):
    sections = lax.axis_size("section")
    my_section = lax.axis_index("section")
    sharding_degree = lax.axis_size("tp")
    slice_breadth = pending_activation.shape[2] // sharding_degree
    col_start = lax.axis_index("tp") * slice_breadth
    lost_at = vanished_hop[0]
    is_pred = my_section == lost_at - 1
    is_next = my_section == lost_at + 1
    is_lost = my_section == lost_at
    w_in = query_key_value_matrices[0]
    w_out = mixing_projection_matrices[0]
    scale_row = normalizer_factors[0]
    entire_source_lines = pending_activation[0]
    x_sh = lax.dynamic_slice_in_dim(entire_source_lines, col_start, slice_breadth, 1)
    blank = jnp.zeros(entire_source_lines.shape, jnp.float32)
    far_in, far_out, far_gain = shifted((w_in, w_out, scale_row), "section", -1)

    def successor_layer(rows_full):
        return attend(layer_norm(rows_full, far_gain), far_in, far_out)

    standby_sh = x_sh
    for tick_index in range(TICKS):
        own_part = attend(layer_norm(entire_source_lines, scale_row), w_in, w_out)
        ya_sh = (
            x_sh.astype(jnp.float32)
            + lax.psum_scatter(own_part, "tp", scatter_dimension=1, tiled=True)
        ).astype(jnp.bfloat16)
        ya_full = lax.all_gather(ya_sh, "tp", axis=1, tiled=True)
        spare_part = (
            successor_layer(ya_full)
            if tick_index == TICKS - 1
            else lax.cond(is_pred, lambda: successor_layer(ya_full), lambda: blank)
        )
        spare_sh = (
            ya_sh.astype(jnp.float32)
            + lax.psum_scatter(spare_part, "tp", scatter_dimension=1, tiled=True)
        ).astype(jnp.bfloat16)
        result_sh = jnp.where(is_pred, spare_sh, ya_sh)
        entering = lax.dynamic_index_in_dim(
            admissible_microbatches, arrival_plan[tick_index], 0, keepdims=False
        )
        send_sh = jnp.where(my_section == sections - 1, entering, result_sh)
        near_rows = shifted(send_sh, "section", 1)
        far_rows = shifted(spare_sh, "section", 2)
        x_sh = jnp.where(is_lost, jnp.zeros_like(far_rows), jnp.where(is_next, far_rows, near_rows))
        entire_source_lines = lax.all_gather(x_sh, "tp", axis=1, tiled=True)
        standby_sh = far_rows
    return (entire_source_lines[None], standby_sh[None])


def solution(mesh):
    placed = (
        P("section", None, None),
        P(None, None, "tp"),
        P(),
        P(),
        P("section", None, None, "tp"),
        P("section", "tp", None),
        P("section", None),
    )
    return jax.shard_map(
        per_device,
        mesh=mesh,
        in_specs=placed,
        out_specs=(P("section", None, None), P("section", None, "tp")),
        check_vma=False,
    )
```

profile of v0, /device:TPU:0, one launch (start us, length us, event | category | flops | bytes accessed | tf_op | source)
XLA Modules:
  0.0 765.0 jit_solution(308551706380850222)
XLA Ops:
  7.2 8.8 %copy.42 = bf16[1,4096,3,256]{1,3,2,0:T(8,128)(2,1)} copy(bf16[1,4096,3,256]{3,1,2,0:T(8,128)(2,1)} %param.15) | data formatting | bytes 12582912 | tf_op args[4]
  16.1 2.4 collective-permute-start.1
  19.9 5.2 convolution_convert_fusion.7
  26.5 1.8 fusion.103
  29.1 68.7 %reduce-scatter.7.cloned.1.call-done = f32[128,512]{1,0:T(8,128)} async-done(((f32[128,4096]{1,0:T(8,128)}), f32[128,512]{1,0:T(8,128)}) %reduce-scatter.7.cloned.1.call-update) | async-done | bytes 262160 | tf_op jit(solution)/shard_map/reduce_scatter | solution.py:87
  97.8 1.6 fusion.86
  100.3 9.4 %collective-permute-done = bf16[4096]{0:T(1024)(128)(2,1)S(1)} collective-permute-done((bf16[4096]{0:T(1024)(128)(2,1)S(1)}, bf16[4096]{0:T(1024)(128)(2,1)S(1)}, u32[]{:S(2)}, u32[]{:S(2)}) %collective-permute-start) | collective-permute-done | bytes 8224 | tf_op jit(solution)/shard_map/ppermute | solution.py:16
  109.7 29.2 %all-gather.7.cloned.1.call-done = bf16[128,4096]{1,0:T(8,128)(2,1)} async-done(((bf16[128,512]{1,0:T(8,128)(2,1)}), bf16[128,4096]{1,0:T(8,128)(2,1)}) %all-gather.7.cloned.1.call-update) | async-done | bytes 1048592 | tf_op jit(solution)/shard_map/all_gather | solution.py:89
  143.7 73.1 %reduce-scatter.9.cloned.1.call-done = f32[128,512]{1,0:T(8,128)} async-done(((f32[128,4096]{1,0:T(8,128)}), f32[128,512]{1,0:T(8,128)}) %reduce-scatter.9.cloned.1.call-update) | async-done | bytes 262160 | tf_op jit(solution)/shard_map/reduce_scatter | solution.py:97
  219.4 3.9 collective-permute-done.3
  225.0 38.5 %all-gather.9.cloned.1.call-done = bf16[128,4096]{1,0:T(8,128)(2,1)} async-done(((bf16[128,512]{1,0:T(8,128)(2,1)}), bf16[128,4096]{1,0:T(8,128)(2,1)}) %all-gather.9.cloned.1.call-update) | async-done | bytes 1048592 | tf_op jit(solution)/shard_map/all_gather | solution.py:107
  265.1 1.7 fusion.48
  266.8 5.0 convolution_convert_fusion.6
  272.6 1.8 fusion.101
  274.5 68.3 %reduce-scatter.11.cloned.1.call-done = f32[128,512]{1,0:T(8,128)} async-done(((f32[128,4096]{1,0:T(8,128)}), f32[128,512]{1,0:T(8,128)}) %reduce-scatter.11.cloned.1.call-update) | async-done | bytes 262160 | tf_op jit(solution)/shard_map/reduce_scatter | solution.py:87
  342.8 1.6 add_convert_fusion.3
  344.5 39.2 %all-gather.11.cloned.1.call-done = bf16[128,4096]{1,0:T(8,128)(2,1)} async-done(((bf16[128,512]{1,0:T(8,128)(2,1)}), bf16[128,4096]{1,0:T(8,128)(2,1)}) %all-gather.11.cloned.1.call-update) | async-done | bytes 1048592 | tf_op jit(solution)/shard_map/all_gather | solution.py:89
  387.3 74.2 %reduce-scatter.13.cloned.1.call-done = f32[128,512]{1,0:T(8,128)} async-done(((f32[128,4096]{1,0:T(8,128)}), f32[128,512]{1,0:T(8,128)}) %reduce-scatter.13.cloned.1.call-update) | async-done | bytes 262160 | tf_op jit(solution)/shard_map/reduce_scatter | solution.py:97
  464.1 4.0 collective-permute-done.5
  469.7 38.5 %all-gather.13.cloned.1.call-done = bf16[128,4096]{1,0:T(8,128)(2,1)} async-done(((bf16[128,512]{1,0:T(8,128)(2,1)}), bf16[128,4096]{1,0:T(8,128)(2,1)}) %all-gather.13.cloned.1.call-update) | async-done | bytes 1048592 | tf_op jit(solution)/shard_map/all_gather | solution.py:107
  509.8 1.7 fusion.45
  511.5 5.0 convolution_convert_fusion.5
  517.3 1.8 fusion.99
  519.2 68.0 %reduce-scatter.15.cloned.1.call-done = f32[128,512]{1,0:T(8,128)} async-done(((f32[128,4096]{1,0:T(8,128)}), f32[128,512]{1,0:T(8,128)}) %reduce-scatter.15.cloned.1.call-update) | async-done | bytes 262160 | tf_op jit(solution)/shard_map/reduce_scatter | solution.py:87
  588.8 39.2 %all-gather.15.cloned.1.call-done = bf16[128,4096]{1,0:T(8,128)(2,1)} async-done(((bf16[128,512]{1,0:T(8,128)(2,1)}), bf16[128,4096]{1,0:T(8,128)(2,1)}) %all-gather.15.cloned.1.call-update) | async-done | bytes 1048592 | tf_op jit(solution)/shard_map/all_gather | solution.py:89
  629.6 1.7 fusion.42
  631.3 5.0 convolution_convert_fusion.4
  637.0 3.4 fusion.120
  642.6 65.9 %reduce-scatter.17.cloned.1.call-done = f32[128,512]{1,0:T(8,128)} async-done(((f32[128,4096]{1,0:T(8,128)}), f32[128,512]{1,0:T(8,128)}) %reduce-scatter.17.cloned.1.call-update) | async-done | bytes 262160 | tf_op jit(solution)/shard_map/reduce_scatter | solution.py:97
  711.1 3.9 collective-permute-done.7
  716.7 38.6 %all-gather.17.cloned.1.call-done = bf16[128,4096]{1,0:T(8,128)(2,1)} async-done(((bf16[128,512]{1,0:T(8,128)(2,1)}), bf16[128,4096]{1,0:T(8,128)(2,1)}) %all-gather.17.cloned.1.call-update) | async-done | bytes 1048592 | tf_op jit(solution)/shard_map/all_gather | solution.py:107
  755.3 2.3 copy.115
  (123 shorter events, 33.5 us)
Async XLA Ops:
  7.2 11.9 %copy-start.15 = (bf16[1,4096]{1,0:T(2,128)(2,1)S(1)}, bf16[1,4096]{1,0:T(2,128)(2,1)}, u32[]{:S(2)}) copy-start(bf16[1,4096]{1,0:T(2,128)(2,1)} %param.17) | copy-start | bytes 24580
  7.2 12.0 %copy-start.1 = (bf16[1,128,4096]{2,1,0:T(8,128)(2,1)S(1)}, bf16[1,128,4096]{2,1,0:T(8,128)(2,1)}, u32[]{:S(2)}) copy-start(bf16[1,128,4096]{2,1,0:T(8,128)(2,1)} %param.11) | copy-start | bytes 3145732
  7.2 90.7 %reduce-scatter.7.cloned.1.call-start = ((), (), s32[]{:S(2)}) async-start(), calls=%async_computation.6 | async-start | bytes 2359296 | tf_op jit(solution)/shard_map/reduce_scatter | solution.py:87
  16.1 122.9 %collective-permute-start.1 = (bf16[4096,3,256]{0,2,1:T(8,128)(2,1)}, bf16[4096,3,256]{0,2,1:T(8,128)(2,1)}, u32[]{:S(2)}, u32[]{:S(2)}) collective-permute-start(bf16[4096,3,256]{0,2,1:T(8,128)(2,1)} %bitcast.141), channel_id=1, source_target_pairs={{0,24},{8,0},{16,8},{24,16},{1,25},{9,1},{17,9},{25,17},{2,26},{10... | collective-permute-start | bytes 18874376 | tf_op jit(solution)/shard_map/ppermute | solution.py:16
  19.8 6.7 copy-start
  28.3 110.6 %all-gather.7.cloned.1.call-start = ((), (), s32[]{:S(2)}) async-start(), calls=%async_computation.7 | async-start | bytes 1179648 | tf_op jit(solution)/shard_map/all_gather | solution.py:89
  28.4 81.3 %collective-permute-start.2 = (bf16[256,4096]{1,0:T(8,128)(2,1)S(1)}, bf16[256,4096]{1,0:T(8,128)(2,1)}, u32[]{:S(2)}, u32[]{:S(2)}) collective-permute-start(bf16[256,4096]{1,0:T(8,128)(2,1)S(1)} %bitcast.140), channel_id=1, source_target_pairs={{0,24},{8,0},{16,8},{24,16},{1,25},{9,1},{17,9},{25,17},{2,26},{10... | collective-permute-start | bytes 6291464 | tf_op jit(solution)/shard_map/ppermute | solution.py:16
  99.5 117.3 %reduce-scatter.9.cloned.1.call-start = ((), (), s32[]{:S(2)}) async-start(), calls=%async_computation.8 | async-start | bytes 2359296 | tf_op jit(solution)/shard_map/reduce_scatter | solution.py:97
  99.6 10.2 %collective-permute-start = (bf16[4096]{0:T(1024)(128)(2,1)S(1)}, bf16[4096]{0:T(1024)(128)(2,1)S(1)}, u32[]{:S(2)}, u32[]{:S(2)}) collective-permute-start(bf16[4096]{0:T(1024)(128)(2,1)S(1)} %reduce.1), channel_id=1, source_target_pairs={{0,24},{8,0},{16,8},{24,16},{1,25},{9,1},{17,9},{25,17},{2,26},{10... | collective-permute-start | bytes 24584 | tf_op jit(solution)/shard_map/ppermute | solution.py:16
  140.5 76.3 %copy-start.7 = (bf16[128,512]{1,0:T(8,128)(2,1)S(1)}, bf16[128,512]{1,0:T(8,128)(2,1)}, u32[]{:S(2)}) copy-start(bf16[128,512]{1,0:T(8,128)(2,1)} %fusion.86) | copy-start | bytes 393220
  140.5 126.3 %copy-start.14 = (f32[4096]{0:T(1024)S(1)}, f32[4096]{0:T(1024)}, u32[]{:S(2)}) copy-start(f32[4096]{0:T(1024)} %copy-done.13) | copy-start | bytes 49156
  140.5 123.1 %all-gather.9.cloned.1.call-start = ((), (), s32[]{:S(2)}) async-start(), calls=%async_computation.9 | async-start | bytes 1179648 | tf_op jit(solution)/shard_map/all_gather | solution.py:107
  217.9 5.5 collective-permute-start.3
  219.4 4.9 collective-permute-start.4
  225.0 117.8 %reduce-scatter.11.cloned.1.call-start = ((), (), s32[]{:S(2)}) async-start(), calls=%async_computation.10 | async-start | bytes 2359296 | tf_op jit(solution)/shard_map/reduce_scatter | solution.py:87
  266.8 5.2 copy-start.16
  274.4 68.4 %copy-start.9 = (bf16[128,512]{1,0:T(8,128)(2,1)S(1)}, bf16[128,512]{1,0:T(8,128)(2,1)}, u32[]{:S(2)}) copy-start(bf16[128,512]{1,0:T(8,128)(2,1)} %select_select_fusion.2) | copy-start | bytes 393220
  274.4 109.3 %all-gather.11.cloned.1.call-start = ((), (), s32[]{:S(2)}) async-start(), calls=%async_computation.11 | async-start | bytes 1179648 | tf_op jit(solution)/shard_map/all_gather | solution.py:89
  344.5 117.0 %reduce-scatter.13.cloned.1.call-start = ((), (), s32[]{:S(2)}) async-start(), calls=%async_computation.12 | async-start | bytes 2359296 | tf_op jit(solution)/shard_map/reduce_scatter | solution.py:97
  385.3 76.2 %copy-start.10 = (bf16[128,512]{1,0:T(8,128)(2,1)S(1)}, bf16[128,512]{1,0:T(8,128)(2,1)}, u32[]{:S(2)}) copy-start(bf16[128,512]{1,0:T(8,128)(2,1)} %add_convert_fusion.3) | copy-start | bytes 393220
  385.3 76.2 %copy-start.12 = (bf16[4,128,512]{2,1,0:T(8,128)(2,1)S(1)}, bf16[4,128,512]{2,1,0:T(8,128)(2,1)}, u32[]{:S(2)}) copy-start(bf16[4,128,512]{2,1,0:T(8,128)(2,1)} %param.12) | copy-start | bytes 1572868
  385.3 122.9 %all-gather.13.cloned.1.call-start = ((), (), s32[]{:S(2)}) async-start(), calls=%async_computation.13 | async-start | bytes 1179648 | tf_op jit(solution)/shard_map/all_gather | solution.py:107
  462.5 5.5 collective-permute-start.5
  464.1 4.9 collective-permute-start.6
  469.7 117.4 %reduce-scatter.15.cloned.1.call-start = ((), (), s32[]{:S(2)}) async-start(), calls=%async_computation.14 | async-start | bytes 2359296 | tf_op jit(solution)/shard_map/reduce_scatter | solution.py:87
  519.1 68.0 %copy-start.8 = (bf16[128,512]{1,0:T(8,128)(2,1)S(1)}, bf16[128,512]{1,0:T(8,128)(2,1)}, u32[]{:S(2)}) copy-start(bf16[128,512]{1,0:T(8,128)(2,1)} %select_select_fusion.1) | copy-start | bytes 393220
  519.1 108.9 %all-gather.15.cloned.1.call-start = ((), (), s32[]{:S(2)}) async-start(), calls=%async_computation.15 | async-start | bytes 1179648 | tf_op jit(solution)/shard_map/all_gather | solution.py:89
  588.8 119.8 %reduce-scatter.17.cloned.1.call-start = ((), (), s32[]{:S(2)}) async-start(), calls=%async_computation.16 | async-start | bytes 2359296 | tf_op jit(solution)/shard_map/reduce_scatter | solution.py:97
  640.5 68.1 %copy-start.11 = (bf16[128,512]{1,0:T(8,128)(2,1)S(1)}, bf16[128,512]{1,0:T(8,128)(2,1)}, u32[]{:S(2)}) copy-start(bf16[128,512]{1,0:T(8,128)(2,1)} %add_convert_fusion.1) | copy-start | bytes 393220
  640.5 114.8 %all-gather.17.cloned.1.call-start = ((), (), s32[]{:S(2)}) async-start(), calls=%async_computation.17 | async-start | bytes 1179648 | tf_op jit(solution)/shard_map/all_gather | solution.py:107
  709.6 5.5 collective-permute-start.7
  711.1 4.9 collective-permute-start.8
  (5 other events, 11.0 us)
Sparse Core Ops, SparseCore 0:
  28.5 69.3 reduce-scatter.6
  100.5 38.4 all-gather.6
  142.5 74.2 reduce-scatter.8
  225.1 38.4 all-gather.8
  274.6 68.2 reduce-scatter.10
  345.3 38.3 all-gather.10
  387.3 74.2 reduce-scatter.12
  469.8 38.4 all-gather.12
  519.2 67.8 reduce-scatter.14
  589.6 38.4 all-gather.14
  640.6 67.8 reduce-scatter.16
  716.8 38.4 all-gather.16
where the time goes:
time: 768 us; the launch traced here: 765 us
  waiting for transfers between devices  666 us (87%)
  matrix products  31.2 us (4%)
  other arithmetic  21.3 us (3%)
  between operations  21.1 us (3%)
  local copies, waits for them, and re-layouts  17.4 us (2%)
  starting transfers between devices  8.37 us (1%)
    reduce_scatter x3, waiting for transfers between devices, per_device(): lax.psum_scatter(spare_part, 'tp', scatter_dimension=1, tiled=True)  213 us
    reduce_scatter x3, waiting for transfers between devices, per_device(): lax.psum_scatter(own_part, 'tp', scatter_dimension=1, tiled=True)  205 us
    all_gather x3, waiting for transfers between devices, per_device(): entire_source_lines = lax.all_gather(x_sh, 'tp', axis=1, tiled=True)  116 us
    all_gather x3, waiting for transfers between devices, per_device(): ya_full = lax.all_gather(ya_sh, 'tp', axis=1, tiled=True)  108 us
    ppermute x9, waiting for transfers between devices, shifted(): return lax.ppermute(value, axis, pairs)  24.1 us
    dot_general x4, matrix products, attend(): jnp.dot(normed, w_in.reshape(w_in.shape[0], 3 * col_count), preferred_ele...  20.2 us
  transfers between devices with their start and end apart: 21, of which 19 were waited for; matrix products, arithmetic and copies ran while one was open for 2% of the time, Pallas kernels for 0%

commit v1 on v0

v1 whole, which is shorter than its diff:
```python
import functools

import jax
import jax.numpy as jnp
from jax import lax
from jax.experimental import pallas as pl
from jax.experimental.pallas import tpu as pltpu
from jax.sharding import PartitionSpec as P

HD = 128
TICKS = 3
NORM_EPS = 1e-05
MESH = pl.DeviceIdType.MESH


def relay_kernel(
    sections, nz, ny,
    lost_ref, plan_ref, pend_ref, pool_ref, win_ref, wout_ref, gain_ref,
    later_ref, standby_ref,
    x_buf, y_buf, acc, qkv, ctx, part, own_part, ry_buf, zs_buf, rz_buf, fwd_buf, last_buf, spare_in,
    ag_zs, ag_zr, ag_ys, ag_yr, rs_zs, rs_zr, rs_ys, rs_yr, sh_s, sh_r,
):
    steps = TICKS + 2
    s = lax.axis_index("section")
    me = lax.axis_index("tp")
    z, y = me // ny, me % ny
    nxt, prv = (s + 1) % sections, (s + sections - 1) % sections
    lost = lost_ref[0]
    devices = nz * ny
    rows, width = x_buf.shape[2], x_buf.shape[3]
    cols = wout_ref.shape[0]
    heads = cols // HD

    def tp_at(dz, dy):
        return ((z + dz + nz) % nz) * ny + (y + dy + ny) % ny

    barrier = pltpu.get_barrier_semaphore()
    for dz in range(1, nz):
        pl.semaphore_signal(barrier, inc=1, device_id={"section": s, "tp": tp_at(dz, 0)}, device_id_type=MESH)
    for dy in range(1, ny):
        pl.semaphore_signal(barrier, inc=1, device_id={"section": s, "tp": tp_at(0, dy)}, device_id_type=MESH)
    pl.semaphore_signal(barrier, inc=1, device_id={"section": nxt, "tp": me}, device_id_type=MESH)
    pl.semaphore_signal(barrier, inc=1, device_id={"section": prv, "tp": me}, device_id_type=MESH)
    pl.semaphore_wait(barrier, nz + ny)

    def copy_to(src, dst, send, recv, section, tp):
        return pltpu.make_async_remote_copy(
            src_ref=src, dst_ref=dst, send_sem=send, recv_sem=recv,
            device_id={"section": section, "tp": tp}, device_id_type=MESH,
        )

    def block_copy(n, slot, send, recv, tp):
        return copy_to(x_buf.at[n, slot], x_buf.at[n, slot], send, recv, s, tp)

    def all_gather(n):
        sends = []
        for dz in range(1, nz):
            sends.append(block_copy(n, me, ag_zs.at[dz], ag_zr.at[n, dz], tp_at(dz, 0)))
            sends[-1].start()
        for dz in range(nz):
            slot = tp_at(-dz, 0)
            if dz:
                block_copy(n, slot, ag_zs.at[dz], ag_zr.at[n, dz], tp_at(dz, 0)).wait_recv()
            for dy in range(1, ny):
                sends.append(block_copy(n, slot, ag_ys.at[dz, dy], ag_yr.at[n, dz, dy], tp_at(0, dy)))
                sends[-1].start()
        for dz in range(nz):
            for dy in range(1, ny):
                slot = tp_at(-dz, -dy)
                block_copy(n, slot, ag_ys.at[dz, dy], ag_yr.at[n, dz, dy], tp_at(0, dy)).wait_recv()
        for copy in sends:
            copy.wait_send()

    def layer(n):
        def add_sum(j, total):
            return total + jnp.sum(x_buf[n, j].astype(jnp.float32), axis=-1, keepdims=True)

        count = float(devices * width)
        mean = lax.fori_loop(0, devices, add_sum, jnp.zeros((rows, 1), jnp.float32)) / count

        def add_square(j, total):
            centered = x_buf[n, j].astype(jnp.float32) - mean
            return total + jnp.sum(centered * centered, axis=-1, keepdims=True)

        var = lax.fori_loop(0, devices, add_square, jnp.zeros((rows, 1), jnp.float32)) / count
        rstd = lax.rsqrt(var + NORM_EPS)
        acc[...] = jnp.zeros_like(acc)

        def project(j, carry):
            at = pl.ds(pl.multiple_of(j * width, 128), width)
            gain = gain_ref[:, at].astype(jnp.float32)
            normed = ((x_buf[n, j].astype(jnp.float32) - mean) * rstd * gain).astype(jnp.bfloat16)
            acc[...] += jnp.dot(normed, win_ref[at, :], preferred_element_type=jnp.float32)
            return carry

        lax.fori_loop(0, devices, project, 0)
        qkv[...] = acc[...].astype(jnp.bfloat16)
        causal = lax.broadcasted_iota(jnp.int32, (rows, rows), 0) >= lax.broadcasted_iota(jnp.int32, (rows, rows), 1)
        for h in range(heads):
            q = qkv[:, h * HD:(h + 1) * HD]
            k = qkv[:, cols + h * HD:cols + (h + 1) * HD]
            v = qkv[:, 2 * cols + h * HD:2 * cols + (h + 1) * HD]
            scores = lax.dot_general(q, k, (((1,), (1,)), ((), ())), preferred_element_type=jnp.float32)
            scores = jnp.where(causal, scores * HD ** (-0.5), -jnp.inf)
            weights = jnp.exp(scores - jnp.max(scores, axis=-1, keepdims=True))
            probs = (weights / jnp.sum(weights, axis=-1, keepdims=True)).astype(jnp.bfloat16)
            ctx[:, h * HD:(h + 1) * HD] = jnp.dot(probs, v, preferred_element_type=jnp.float32).astype(jnp.bfloat16)

        def partial_for(tp):
            at = pl.ds(pl.multiple_of(tp * width, 128), width)
            return jnp.dot(ctx[...], wout_ref[:, at], preferred_element_type=jnp.float32)

        order = list(range(1, nz)) + [0]
        sends, got = [], {}
        for dz in order:
            for dy in range(1, ny):
                part[dy - 1, dz] = partial_for(tp_at(dz, dy)).astype(jnp.bfloat16)
                got[dz, dy] = copy_to(part.at[dy - 1, dz], ry_buf.at[n, dy - 1, dz],
                                      rs_ys.at[dz, dy], rs_yr.at[n, dz, dy], s, tp_at(0, dy))
                got[dz, dy].start()
        for dz in order:
            own_part[dz] = partial_for(tp_at(dz, 0))
        for dz in order:
            total = own_part[dz]
            for dy in range(1, ny):
                got[dz, dy].wait_recv()
                total = total + ry_buf[n, dy - 1, dz].astype(jnp.float32)
            if dz:
                zs_buf[dz - 1] = total.astype(jnp.bfloat16)
                sends.append(copy_to(zs_buf.at[dz - 1], rz_buf.at[n, dz - 1], rs_zs.at[dz], rs_zr.at[n, dz],
                                     s, tp_at(dz, 0)))
                sends[-1].start()
            else:
                own_part[0] = total
        total = own_part[0]
        for copy in sends:
            copy.wait_recv()
        for dz in range(1, nz):
            total = total + rz_buf[n, dz - 1].astype(jnp.float32)
        y_buf[n] = (x_buf[n, me].astype(jnp.float32) + total).astype(jnp.bfloat16)
        for copy in list(got.values()) + sends:
            copy.wait_send()

    def needed(section, n):
        tail = (n <= TICKS) | (section > 2) | (section == 0)
        live = (section + TICKS - 1 >= n) | ((section == 0) & (n == TICKS + 1))
        if sections <= TICKS + 1:
            live = live & ((section != sections - 1) | (n != TICKS - 1))
        return live & tail

    def passes(section, n):
        return needed(section, n) & (n > 0) & ((section > 0) | (n == TICKS + 1))

    def shift_copy(n):
        return copy_to(fwd_buf, x_buf.at[n, me], sh_s.at[0], sh_r.at[n], nxt, me)

    def pick(cond, a, b):
        return jnp.where(jnp.full(a.shape, cond), a, b)

    def own_rows():
        settled = pick((s < lost) | (s - TICKS + 1 > lost), y_buf[TICKS - 1], y_buf[TICKS])
        return pick(s == lost, y_buf[0], settled)

    def step(n, carry):
        @pl.when(needed(s, n))
        def _():
            @pl.when(n == 0)
            def _():
                for j in range(devices):
                    rows_j = pend_ref[0, :, j * width:(j + 1) * width]
                    x_buf[0, j] = pick(s == lost, jnp.zeros_like(rows_j), rows_j)

            @pl.when(passes(s, n))
            def _():
                shift_copy(n).wait_recv()

            @pl.when(n > 0)
            def _():
                @pl.when(jnp.logical_not(passes(s, n)))
                def _():
                    x_buf[n, me] = pool_ref[plan_ref[n - 1]]

                all_gather(n)

            layer(n)

        @pl.when(jnp.logical_not(needed(s, n)))
        def _():
            y_buf[n] = jnp.zeros((rows, width), jnp.bfloat16)

        @pl.when((n < steps - 1) & passes(nxt, n + 1))
        def _():
            fwd_buf[...] = y_buf[n]

            @pl.when((n == TICKS) & (s == sections - 1))
            def _():
                fwd_buf[...] = own_rows()

            copy = shift_copy(n + 1)
            copy.start()
            copy.wait_send()

        return carry

    lax.fori_loop(0, steps, step, 0)

    settled = pick((s - 1 < lost) | (s - TICKS > lost), y_buf[TICKS], y_buf[TICKS + 1])
    spare = pick(s - 1 == lost, y_buf[1], settled)
    spare = pick(s == 0, y_buf[TICKS + 1], spare)
    final = pick(s == lost, spare, own_rows())
    final = pick(nxt == 0, pool_ref[plan_ref[TICKS - 1]], final)
    last_buf[0] = pick(nxt == lost, jnp.zeros_like(final), final)
    last_buf[1] = spare
    out_copy = copy_to(last_buf.at[0], x_buf.at[steps, me], sh_s.at[0], sh_r.at[steps], nxt, me)
    spare_copy = copy_to(last_buf.at[1], spare_in, sh_s.at[1], sh_r.at[0], nxt, me)
    out_copy.start()
    spare_copy.start()
    out_copy.wait_recv()
    all_gather(steps)
    for j in range(devices):
        later_ref[0, :, j * width:(j + 1) * width] = x_buf[steps, j]
    spare_copy.wait_recv()
    standby_ref[0] = spare_in[...]
    out_copy.wait_send()
    spare_copy.wait_send()


def solution(mesh):
    sections, devices = mesh.shape["section"], mesh.shape["tp"]
    ny = 1
    while (2 * ny) * (2 * ny) <= devices and devices % (2 * ny) == 0:
        ny *= 2
    nz = devices // ny

    def per_device(pend, pool, plan, lost, win, wout, gain):
        rows, hidden = pend.shape[1], pend.shape[2]
        width = hidden // devices
        cols = win.shape[3]
        slots = TICKS + 3
        win = win.reshape(hidden, 3 * cols)
        vmem = pl.BlockSpec(memory_space=pltpu.VMEM)
        smem = pl.BlockSpec(memory_space=pltpu.SMEM)
        bf = functools.partial(pltpu.VMEM, dtype=jnp.bfloat16)
        dma = pltpu.SemaphoreType.DMA
        return pl.pallas_call(
            functools.partial(relay_kernel, sections, nz, ny),
            out_shape=(
                jax.ShapeDtypeStruct((1, rows, hidden), jnp.bfloat16),
                jax.ShapeDtypeStruct((1, rows, width), jnp.bfloat16),
            ),
            in_specs=[smem, smem] + [vmem] * 5,
            out_specs=(vmem, vmem),
            scratch_shapes=[
                bf((slots, devices, rows, width)),
                bf((slots, rows, width)),
                pltpu.VMEM((rows, 3 * cols), jnp.float32),
                bf((rows, 3 * cols)),
                bf((rows, cols)),
                bf((ny - 1, nz, rows, width)),
                pltpu.VMEM((nz, rows, width), jnp.float32),
                bf((slots, ny - 1, nz, rows, width)),
                bf((nz - 1, rows, width)),
                bf((slots, nz - 1, rows, width)),
                bf((rows, width)),
                bf((2, rows, width)),
                bf((rows, width)),
                dma((nz,)), dma((slots, nz)), dma((nz, ny)), dma((slots, nz, ny)),
                dma((nz,)), dma((slots, nz)), dma((nz, ny)), dma((slots, nz, ny)),
                dma((2,)), dma((slots,)),
            ],
            compiler_params=pltpu.CompilerParams(
                collective_id=0, has_side_effects=True, vmem_limit_bytes=60 * 1024 * 1024
            ),
        )(lost, plan, pend, pool, win, wout[0], gain)

    placed = (
        P("section", None, None),
        P(None, None, "tp"),
        P(),
        P(),
        P("section", None, None, "tp"),
        P("section", "tp", None),
        P("section", None),
    )
    return jax.shard_map(
        per_device,
        mesh=mesh,
        in_specs=placed,
        out_specs=(P("section", None, None), P("section", None, "tp")),
        check_vma=False,
    )
```

time: 768 us -> 234 us (0.30)
  waiting for transfers between devices: 666 us -> 0 us
  Pallas kernels: 0 us -> 211 us
  matrix products: 31.2 us -> 0 us
  other arithmetic: 21.3 us -> 0 us
  between operations: 21.1 us -> 1.29 us
  starting transfers between devices: 8.37 us -> 0 us
    reduce_scatter x6 -> x0, waiting for transfers between devices: 418 us -> none  [the longest x3 213 us: per_device(): lax.psum_scatter(spare_part, 'tp', scatter_dimension=1, tiled=True)]
    all_gather x6 -> x0, waiting for transfers between devices: 223 us -> none  [the longest x3 116 us: per_device(): entire_source_lines = lax.all_gather(x_sh, 'tp', axis=1, tiled=True)]
    pallas_call x0 -> x1, Pallas kernels: none -> 211 us  [per_device(): pl.pallas_call(functools.partial(relay_kernel, sections, nz, ny), out_sha...]
    dot_general x16 -> x0, matrix products: 31.2 us -> none  [the longest x4 20.2 us: attend(): jnp.dot(normed, w_in.reshape(w_in.shape[0], 3 * col_count), preferred_ele...]
    ppermute x9 -> x0, waiting for transfers between devices: 24.1 us -> none  [shifted(): return lax.ppermute(value, axis, pairs)]
    reduce_sum x8 -> x0, other arithmetic: 10.2 us -> none  [the longest x4 5.39 us: layer_norm(): row_var = jnp.mean(centered * centered, axis=-1, keepdims=True)]
    reshape x4 -> x1, local copies, waits for them, and re-layouts: 0.2 us -> 8.67 us  [per_device(): win = win.reshape(hidden, 3 * cols)]
    ppermute x9 -> x0, starting transfers between devices: 7.88 us -> none  [shifted(): return lax.ppermute(value, axis, pairs)]
  transfers between devices with their start and end apart: 21 -> 0, of which waited for: 19 -> 0; matrix products, arithmetic and copies ran while one was open for 2% -> 0% of each run, Pallas kernels for 0% -> 0%
where the time goes in v1:
time: 234 us; the launch traced here: 233 us
  Pallas kernels  211 us (90%)
  local copies, waits for them, and re-layouts  21.3 us (9%)
    pallas_call x1, Pallas kernels, per_device(): pl.pallas_call(functools.partial(relay_kernel, sections, nz, ny), out_sha...  211 us
    unnamed x3, local copies, waits for them, and re-layouts  12.6 us
    reshape x1, local copies, waits for them, and re-layouts, per_device(): win = win.reshape(hidden, 3 * cols)  8.67 us

profile of v1, /device:TPU:0, one launch (start us, length us, event | category | flops | bytes accessed | tf_op | source)
XLA Modules:
  0.0 233.5 jit_solution(1661677134017384579)
XLA Ops:
  0.6 8.8 %copy.10 = bf16[1,4096,3,256]{1,3,2,0:T(8,128)(2,1)} copy(bf16[1,4096,3,256]{3,1,2,0:T(8,128)(2,1)} %param.11) | data formatting | bytes 12582912 | tf_op args[4]
  9.4 8.7 %copy.11.win_ref = bf16[4096,768]{1,0:T(8,128)(2,1)} copy(bf16[4096,768]{0,1:T(8,128)(2,1)} %bitcast.2) | data formatting | bytes 12582912 | tf_op jit(solution)/shard_map/reshape | solution.py:240
  18.7 210.9 %shard_map.86 = (bf16[1,128,4096]{2,1,0:T(8,128)(2,1)}, bf16[1,128,512]{2,1,0:T(8,128)(2,1)}) custom-call(s32[1]{0:T(128)S(6)} %copy.14.lost_ref, s32[4]{0:T(128)} %plan_ref.1, bf16[1,128,4096]{2,1,0:T(8,128)(2,1)} %pend_ref.1, bf16[4,128,512]{2,1,0:T(8,128)(2,1)} %pool_ref.1, bf16[4096,768]{1,0:T(8,128)(2,1)} %copy.11.win_ref, bf16[256,4096]{1,0:T(8,128)(2,1)} %bitcast.3, ...), custom_call_target="tpu_custom_call" | custom-call | tf_op jit(solution)/shard_map/pallas_call | solution.py:245
  229.6 2.3 copy.15
  231.9 1.6 copy.16

commit v2 on v1

--- a/solution.py
+++ b/solution.py
@@ -31,8 +31,16 @@
     cols = wout_ref.shape[0]
     heads = cols // HD
 
+    def partner(at, mask):
+        bit = 1
+        while bit <= mask:
+            if mask & bit:
+                at = at + bit - 2 * bit * ((at // bit) % 2)
+            bit *= 2
+        return at
+
     def tp_at(dz, dy):
-        return ((z + dz + nz) % nz) * ny + (y + dy + ny) % ny
+        return partner(z, dz) * ny + partner(y, dy)
 
     barrier = pltpu.get_barrier_semaphore()
     for dz in range(1, nz):
@@ -52,24 +60,33 @@
     def block_copy(n, slot, send, recv, tp):
         return copy_to(x_buf.at[n, slot], x_buf.at[n, slot], send, recv, s, tp)
 
-    def all_gather(n):
-        sends = []
+    def z_copy(n, dz, slot):
+        return block_copy(n, slot, ag_zs.at[dz], ag_zr.at[n, dz], tp_at(dz, 0))
+
+    def y_copy(n, dz, dy, slot):
+        return block_copy(n, slot, ag_ys.at[dz, dy], ag_yr.at[n, dz, dy], tp_at(0, dy))
+
+    def ag_start(n):
         for dz in range(1, nz):
-            sends.append(block_copy(n, me, ag_zs.at[dz], ag_zr.at[n, dz], tp_at(dz, 0)))
-            sends[-1].start()
+            z_copy(n, dz, me).start()
+        for dy in range(1, ny):
+            y_copy(n, 0, dy, me).start()
+
+    def ag_forward(n):
+        for dz in range(1, nz):
+            z_copy(n, dz, tp_at(dz, 0)).wait_recv()
+            for dy in range(1, ny):
+                y_copy(n, dz, dy, tp_at(dz, 0)).start()
+
+    def ag_finish(n):
         for dz in range(nz):
-            slot = tp_at(-dz, 0)
-            if dz:
-                block_copy(n, slot, ag_zs.at[dz], ag_zr.at[n, dz], tp_at(dz, 0)).wait_recv()
-            for dy in range(1, ny):
-                sends.append(block_copy(n, slot, ag_ys.at[dz, dy], ag_yr.at[n, dz, dy], tp_at(0, dy)))
-                sends[-1].start()
+            for dy in range(1, ny):
+                y_copy(n, dz, dy, tp_at(dz, dy)).wait_recv()
+        for dz in range(1, nz):
+            z_copy(n, dz, me).wait_send()
         for dz in range(nz):
             for dy in range(1, ny):
-                slot = tp_at(-dz, -dy)
-                block_copy(n, slot, ag_ys.at[dz, dy], ag_yr.at[n, dz, dy], tp_at(0, dy)).wait_recv()
-        for copy in sends:
-            copy.wait_send()
+                y_copy(n, dz, dy, tp_at(dz, 0)).wait_send()
 
     def layer(n):
         def add_sum(j, total):
@@ -90,7 +107,9 @@
             at = pl.ds(pl.multiple_of(j * width, 128), width)
             gain = gain_ref[:, at].astype(jnp.float32)
             normed = ((x_buf[n, j].astype(jnp.float32) - mean) * rstd * gain).astype(jnp.bfloat16)
-            acc[...] += jnp.dot(normed, win_ref[at, :], preferred_element_type=jnp.float32)
+            acc[...] += lax.dot_general(
+                normed, win_ref[:, at], (((1,), (1,)), ((), ())), preferred_element_type=jnp.float32
+            )
             return carry
 
         lax.fori_loop(0, devices, project, 0)
@@ -110,7 +129,7 @@
             at = pl.ds(pl.multiple_of(tp * width, 128), width)
             return jnp.dot(ctx[...], wout_ref[:, at], preferred_element_type=jnp.float32)
 
-        order = list(range(1, nz)) + [0]
+        order = list(range(nz - 1, -1, -1))
         sends, got = [], {}
         for dz in order:
             for dy in range(1, ny):
@@ -132,6 +151,14 @@
                 sends[-1].start()
             else:
                 own_part[0] = total
+        @pl.when((s == 0) & (n < TICKS - 1))
+        def _():
+            ag_forward(n + 1)
+
+        @pl.when(n == TICKS + 1)
+        def _():
+            ag_forward(steps)
+
         total = own_part[0]
         for copy in sends:
             copy.wait_recv()
@@ -161,6 +188,8 @@
         settled = pick((s < lost) | (s - TICKS + 1 > lost), y_buf[TICKS - 1], y_buf[TICKS])
         return pick(s == lost, y_buf[0], settled)
 
+    out_copy = copy_to(last_buf.at[0], x_buf.at[steps, me], sh_s.at[1], sh_r.at[steps], nxt, me)
+
     def step(n, carry):
         @pl.when(needed(s, n))
         def _():
@@ -173,20 +202,34 @@
             @pl.when(passes(s, n))
             def _():
                 shift_copy(n).wait_recv()
+                ag_start(n)
+                ag_forward(n)
 
             @pl.when(n > 0)
             def _():
-                @pl.when(jnp.logical_not(passes(s, n)))
-                def _():
-                    x_buf[n, me] = pool_ref[plan_ref[n - 1]]
-
-                all_gather(n)
+                ag_finish(n)
+
+            @pl.when((s == 0) & (n < TICKS - 1))
+            def _():
+                x_buf[n + 1, me] = pool_ref[plan_ref[n]]
+                ag_start(n + 1)
+
+            @pl.when(n == TICKS + 1)
+            def _():
+                out_copy.wait_recv()
+                ag_start(steps)
 
             layer(n)
 
         @pl.when(jnp.logical_not(needed(s, n)))
         def _():
             y_buf[n] = jnp.zeros((rows, width), jnp.bfloat16)
+
+            @pl.when(n == TICKS + 1)
+            def _():
+                out_copy.wait_recv()
+                ag_start(steps)
+                ag_forward(steps)
 
         @pl.when((n < steps - 1) & passes(nxt, n + 1))
         def _():
@@ -200,6 +243,13 @@
             copy.start()
             copy.wait_send()
 
+        @pl.when(n == TICKS)
+        def _():
+            final = pick(s == lost, y_buf[TICKS], own_rows())
+            final = pick(nxt == 0, pool_ref[plan_ref[TICKS - 1]], final)
+            last_buf[0] = pick(nxt == lost, jnp.zeros_like(final), final)
+            out_copy.start()
+
         return carry
 
     lax.fori_loop(0, steps, step, 0)
@@ -207,16 +257,10 @@
     settled = pick((s - 1 < lost) | (s - TICKS > lost), y_buf[TICKS], y_buf[TICKS + 1])
     spare = pick(s - 1 == lost, y_buf[1], settled)
     spare = pick(s == 0, y_buf[TICKS + 1], spare)
-    final = pick(s == lost, spare, own_rows())
-    final = pick(nxt == 0, pool_ref[plan_ref[TICKS - 1]], final)
-    last_buf[0] = pick(nxt == lost, jnp.zeros_like(final), final)
     last_buf[1] = spare
-    out_copy = copy_to(last_buf.at[0], x_buf.at[steps, me], sh_s.at[0], sh_r.at[steps], nxt, me)
-    spare_copy = copy_to(last_buf.at[1], spare_in, sh_s.at[1], sh_r.at[0], nxt, me)
-    out_copy.start()
+    spare_copy = copy_to(last_buf.at[1], spare_in, sh_s.at[0], sh_r.at[0], nxt, me)
     spare_copy.start()
-    out_copy.wait_recv()
-    all_gather(steps)
+    ag_finish(steps)
     for j in range(devices):
         later_ref[0, :, j * width:(j + 1) * width] = x_buf[steps, j]
     spare_copy.wait_recv()
@@ -237,7 +281,7 @@
         width = hidden // devices
         cols = win.shape[3]
         slots = TICKS + 3
-        win = win.reshape(hidden, 3 * cols)
+        win = jnp.transpose(win[0], (1, 2, 0)).reshape(3 * cols, hidden)
         vmem = pl.BlockSpec(memory_space=pltpu.VMEM)
         smem = pl.BlockSpec(memory_space=pltpu.SMEM)
         bf = functools.partial(pltpu.VMEM, dtype=jnp.bfloat16)

time: 234 us -> 196 us (0.84)
  Pallas kernels: 211 us -> 182 us
  local copies, waits for them, and re-layouts: 21.3 us -> 12.7 us
    pallas_call x1, Pallas kernels: 211 us -> 182 us  [per_device(): pl.pallas_call(functools.partial(relay_kernel, sections, nz, ny), out_sha...]
    transpose x0 -> x1, local copies, waits for them, and re-layouts: none -> 8.82 us  [per_device(): win = jnp.transpose(win[0], (1, 2, 0)).reshape(3 * cols, hidden)]
    unnamed x3 -> x2, local copies, waits for them, and re-layouts: 12.6 us -> 3.85 us
    reshape x1 -> x0, local copies, waits for them, and re-layouts: 8.67 us -> none  [per_device(): win = win.reshape(hidden, 3 * cols)]
where the time goes in v2:
time: 196 us
  Pallas kernels  182 us (93%)
  local copies, waits for them, and re-layouts  12.7 us (6%)
    pallas_call x1, Pallas kernels, per_device(): pl.pallas_call(functools.partial(relay_kernel, sections, nz, ny), out_sha...  182 us
    transpose x1, local copies, waits for them, and re-layouts, per_device(): win = jnp.transpose(win[0], (1, 2, 0)).reshape(3 * cols, hidden)  8.82 us

profile of v2, /device:TPU:0, one launch (start us, length us, event | category | flops | bytes accessed | tf_op | source)
XLA Modules:
  0.0 195.9 jit_solution(3541536352116071664)
XLA Ops:
  1.3 8.8 %copy.9 = bf16[3,256,4096]{2,1,0:T(8,128)(2,1)} copy(bf16[3,256,4096]{1,2,0:T(8,128)(2,1)} %bitcast.6) | data formatting | bytes 12582912 | tf_op jit(solution)/shard_map/transpose | solution.py:284
  10.1 182.0 %shard_map.86 = (bf16[1,128,4096]{2,1,0:T(8,128)(2,1)}, bf16[1,128,512]{2,1,0:T(8,128)(2,1)}) custom-call(s32[1]{0:T(128)S(6)} %copy.12.lost_ref, s32[4]{0:T(128)} %plan_ref.1, bf16[1,128,4096]{2,1,0:T(8,128)(2,1)} %pend_ref.1, bf16[4,128,512]{2,1,0:T(8,128)(2,1)} %pool_ref.1, bf16[768,4096]{1,0:T(8,128)(2,1)} %bitcast.5, bf16[256,4096]{1,0:T(8,128)(2,1)} %bitcast.7, ...), custom_call_target="tpu_custom_call" | custom-call | tf_op jit(solution)/shard_map/pallas_call | solution.py:289
  192.1 2.3 %copy.13 = bf16[1,128,4096]{2,1,0:T(8,128)(2,1)} copy(bf16[1,128,4096]{2,1,0:T(8,128)(2,1)} %get-tuple-element.4) | data formatting | bytes 2097152
  194.4 1.6 copy.14

commit v3 on v2

--- a/solution.py
+++ b/solution.py
@@ -15,9 +15,9 @@
 
 def relay_kernel(
     sections, nz, ny,
-    lost_ref, plan_ref, pend_ref, pool_ref, win_ref, wout_ref, gain_ref,
+    lost_ref, plan_ref, pend_ref, pool_ref, win_hbm, wout_hbm, gain_ref,
     later_ref, standby_ref,
-    x_buf, y_buf, acc, qkv, ctx, part, own_part, ry_buf, zs_buf, rz_buf, fwd_buf, last_buf, spare_in,
+    win_ref, wout_ref, w_sem, x_buf, y_buf, acc, qkv, ctx, part, own_part, ry_buf, zs_buf, rz_buf, fwd_buf, last_buf, spare_in,
     ag_zs, ag_zr, ag_ys, ag_yr, rs_zs, rs_zr, rs_ys, rs_yr, sh_s, sh_r,
 ):
     steps = TICKS + 2
@@ -42,6 +42,10 @@
     def tp_at(dz, dy):
         return partner(z, dz) * ny + partner(y, dy)
 
+    win_copy = pltpu.make_async_copy(win_hbm, win_ref, w_sem.at[0])
+    wout_copy = pltpu.make_async_copy(wout_hbm, wout_ref, w_sem.at[1])
+    win_copy.start()
+    wout_copy.start()
     barrier = pltpu.get_barrier_semaphore()
     for dz in range(1, nz):
         pl.semaphore_signal(barrier, inc=1, device_id={"section": s, "tp": tp_at(dz, 0)}, device_id_type=MESH)
@@ -101,15 +105,22 @@
 
         var = lax.fori_loop(0, devices, add_square, jnp.zeros((rows, 1), jnp.float32)) / count
         rstd = lax.rsqrt(var + NORM_EPS)
+
+        @pl.when(n == 0)
+        def _():
+            win_copy.wait()
+            wout_copy.wait()
+
         acc[...] = jnp.zeros_like(acc)
 
         def project(j, carry):
             at = pl.ds(pl.multiple_of(j * width, 128), width)
             gain = gain_ref[:, at].astype(jnp.float32)
             normed = ((x_buf[n, j].astype(jnp.float32) - mean) * rstd * gain).astype(jnp.bfloat16)
-            acc[...] += lax.dot_general(
-                normed, win_ref[:, at], (((1,), (1,)), ((), ())), preferred_element_type=jnp.float32
-            )
+            for i in range(3):
+                acc[:, i * cols:(i + 1) * cols] += jnp.dot(
+                    normed, win_ref[i, at, :], preferred_element_type=jnp.float32
+                )
             return carry
 
         lax.fori_loop(0, devices, project, 0)
@@ -281,9 +292,10 @@
         width = hidden // devices
         cols = win.shape[3]
         slots = TICKS + 3
-        win = jnp.transpose(win[0], (1, 2, 0)).reshape(3 * cols, hidden)
+        win = jnp.transpose(win[0], (1, 0, 2))
         vmem = pl.BlockSpec(memory_space=pltpu.VMEM)
         smem = pl.BlockSpec(memory_space=pltpu.SMEM)
+        hbm = pl.BlockSpec(memory_space=pl.ANY)
         bf = functools.partial(pltpu.VMEM, dtype=jnp.bfloat16)
         dma = pltpu.SemaphoreType.DMA
         return pl.pallas_call(
@@ -292,9 +304,12 @@
                 jax.ShapeDtypeStruct((1, rows, hidden), jnp.bfloat16),
                 jax.ShapeDtypeStruct((1, rows, width), jnp.bfloat16),
             ),
-            in_specs=[smem, smem] + [vmem] * 5,
+            in_specs=[smem, smem, vmem, vmem, hbm, hbm, vmem],
             out_specs=(vmem, vmem),
             scratch_shapes=[
+                bf((3, hidden, cols)),
+                bf((cols, hidden)),
+                dma((2,)),
                 bf((slots, devices, rows, width)),
                 bf((slots, rows, width)),
                 pltpu.VMEM((rows, 3 * cols), jnp.float32),

time: 196 us -> 180 us (0.918)
  local copies, waits for them, and re-layouts: 12.7 us -> 3.85 us
  Pallas kernels: 182 us -> 175 us
    transpose x1 -> x0, local copies, waits for them, and re-layouts: 8.82 us -> none  [per_device(): win = jnp.transpose(win[0], (1, 2, 0)).reshape(3 * cols, hidden)]
    pallas_call x1, Pallas kernels: 182 us -> 175 us  [per_device(): pl.pallas_call(functools.partial(relay_kernel, sections, nz, ny), out_sha...]
where the time goes in v3:
time: 180 us
  Pallas kernels  175 us (97%)
  local copies, waits for them, and re-layouts  3.85 us (2%)
    pallas_call x1, Pallas kernels, per_device(): pl.pallas_call(functools.partial(relay_kernel, sections, nz, ny), out_sha...  175 us
    unnamed x2, local copies, waits for them, and re-layouts  3.85 us

profile of v3, /device:TPU:0, one launch (start us, length us, event | category | flops | bytes accessed | tf_op | source)
XLA Modules:
  0.0 179.8 jit_solution(15908017588620112249)
XLA Ops:
  1.3 174.7 %shard_map.86 = (bf16[1,128,4096]{2,1,0:T(8,128)(2,1)}, bf16[1,128,512]{2,1,0:T(8,128)(2,1)}) custom-call(s32[1]{0:T(128)S(6)} %copy.11.lost_ref, s32[4]{0:T(128)} %plan_ref.1, bf16[1,128,4096]{2,1,0:T(8,128)(2,1)} %pend_ref.1, bf16[4,128,512]{2,1,0:T(8,128)(2,1)} %pool_ref.1, bf16[3,4096,256]{2,1,0:T(8,128)(2,1)} %bitcast.4, bf16[256,4096]{1,0:T(8,128)(2,1)} %bitcast.5, ...), custom_call_target="tpu_custom_call" | custom-call | tf_op jit(solution)/shard_map/pallas_call | solution.py:301
  176.0 2.3 %copy.12 = bf16[1,128,4096]{2,1,0:T(8,128)(2,1)} copy(bf16[1,128,4096]{2,1,0:T(8,128)(2,1)} %get-tuple-element.4) | data formatting | bytes 2097152
  178.3 1.6 copy.13

commit v4 on v3

--- a/solution.py
+++ b/solution.py
@@ -11,6 +11,7 @@
 TICKS = 3
 NORM_EPS = 1e-05
 MESH = pl.DeviceIdType.MESH
+PIECES = 2
 
 
 def relay_kernel(
@@ -61,36 +62,43 @@
             device_id={"section": section, "tp": tp}, device_id_type=MESH,
         )
 
-    def block_copy(n, slot, send, recv, tp):
-        return copy_to(x_buf.at[n, slot], x_buf.at[n, slot], send, recv, s, tp)
-
-    def z_copy(n, dz, slot):
-        return block_copy(n, slot, ag_zs.at[dz], ag_zr.at[n, dz], tp_at(dz, 0))
-
-    def y_copy(n, dz, dy, slot):
-        return block_copy(n, slot, ag_ys.at[dz, dy], ag_yr.at[n, dz, dy], tp_at(0, dy))
+    def span(h):
+        return pl.ds(h * (rows // PIECES), rows // PIECES)
+
+    def block_copy(n, slot, h, send, recv, tp):
+        return copy_to(x_buf.at[n, slot, span(h)], x_buf.at[n, slot, span(h)], send, recv, s, tp)
+
+    def z_copy(n, h, dz, slot):
+        return block_copy(n, slot, h, ag_zs.at[h, dz], ag_zr.at[n, h, dz], tp_at(dz, 0))
+
+    def y_copy(n, h, dz, dy, slot):
+        return block_copy(n, slot, h, ag_ys.at[h, dz, dy], ag_yr.at[n, h, dz, dy], tp_at(0, dy))
 
     def ag_start(n):
         for dz in range(1, nz):
-            z_copy(n, dz, me).start()
+            for h in range(PIECES):
+                z_copy(n, h, dz, me).start()
         for dy in range(1, ny):
-            y_copy(n, 0, dy, me).start()
+            for h in range(PIECES):
+                y_copy(n, h, 0, dy, me).start()
 
     def ag_forward(n):
         for dz in range(1, nz):
-            z_copy(n, dz, tp_at(dz, 0)).wait_recv()
-            for dy in range(1, ny):
-                y_copy(n, dz, dy, tp_at(dz, 0)).start()
+            for h in range(PIECES):
+                z_copy(n, h, dz, tp_at(dz, 0)).wait_recv()
+                for dy in range(1, ny):
+                    y_copy(n, h, dz, dy, tp_at(dz, 0)).start()
 
     def ag_finish(n):
-        for dz in range(nz):
-            for dy in range(1, ny):
-                y_copy(n, dz, dy, tp_at(dz, dy)).wait_recv()
-        for dz in range(1, nz):
-            z_copy(n, dz, me).wait_send()
-        for dz in range(nz):
-            for dy in range(1, ny):
-                y_copy(n, dz, dy, tp_at(dz, 0)).wait_send()
+        for h in range(PIECES):
+            for dz in range(nz):
+                for dy in range(1, ny):
+                    y_copy(n, h, dz, dy, tp_at(dz, dy)).wait_recv()
+            for dz in range(1, nz):
+                z_copy(n, h, dz, me).wait_send()
+            for dz in range(nz):
+                for dy in range(1, ny):
+                    y_copy(n, h, dz, dy, tp_at(dz, 0)).wait_send()
 
     def layer(n):
         def add_sum(j, total):
@@ -145,23 +153,26 @@
         for dz in order:
             for dy in range(1, ny):
                 part[dy - 1, dz] = partial_for(tp_at(dz, dy)).astype(jnp.bfloat16)
-                got[dz, dy] = copy_to(part.at[dy - 1, dz], ry_buf.at[n, dy - 1, dz],
-                                      rs_ys.at[dz, dy], rs_yr.at[n, dz, dy], s, tp_at(0, dy))
-                got[dz, dy].start()
+                for h in range(PIECES):
+                    got[dz, dy, h] = copy_to(part.at[dy - 1, dz, span(h)], ry_buf.at[n, dy - 1, dz, span(h)],
+                                             rs_ys.at[h, dz, dy], rs_yr.at[n, h, dz, dy], s, tp_at(0, dy))
+                    got[dz, dy, h].start()
         for dz in order:
             own_part[dz] = partial_for(tp_at(dz, 0))
         for dz in order:
-            total = own_part[dz]
-            for dy in range(1, ny):
-                got[dz, dy].wait_recv()
-                total = total + ry_buf[n, dy - 1, dz].astype(jnp.float32)
-            if dz:
-                zs_buf[dz - 1] = total.astype(jnp.bfloat16)
-                sends.append(copy_to(zs_buf.at[dz - 1], rz_buf.at[n, dz - 1], rs_zs.at[dz], rs_zr.at[n, dz],
-                                     s, tp_at(dz, 0)))
-                sends[-1].start()
-            else:
-                own_part[0] = total
+            for h in range(PIECES):
+                total = own_part[dz, span(h)]
+                for dy in range(1, ny):
+                    got[dz, dy, h].wait_recv()
+                    total = total + ry_buf[n, dy - 1, dz, span(h)].astype(jnp.float32)
+                if dz:
+                    zs_buf[dz - 1, span(h)] = total.astype(jnp.bfloat16)
+                    sends.append(copy_to(zs_buf.at[dz - 1, span(h)], rz_buf.at[n, dz - 1, span(h)],
+                                         rs_zs.at[h, dz], rs_zr.at[n, h, dz], s, tp_at(dz, 0)))
+                    sends[-1].start()
+                else:
+                    own_part[0, span(h)] = total
+
         @pl.when((s == 0) & (n < TICKS - 1))
         def _():
             ag_forward(n + 1)
@@ -323,8 +334,8 @@
                 bf((rows, width)),
                 bf((2, rows, width)),
                 bf((rows, width)),
-                dma((nz,)), dma((slots, nz)), dma((nz, ny)), dma((slots, nz, ny)),
-                dma((nz,)), dma((slots, nz)), dma((nz, ny)), dma((slots, nz, ny)),
+                dma((PIECES, nz)), dma((slots, PIECES, nz)), dma((PIECES, nz, ny)), dma((slots, PIECES, nz, ny)),
+                dma((PIECES, nz)), dma((slots, PIECES, nz)), dma((PIECES, nz, ny)), dma((slots, PIECES, nz, ny)),
                 dma((2,)), dma((slots,)),
             ],
             compiler_params=pltpu.CompilerParams(

time: 180 us -> 174 us (0.967)
  Pallas kernels: 175 us -> 169 us
    pallas_call x1, Pallas kernels: 175 us -> 169 us  [per_device(): pl.pallas_call(functools.partial(relay_kernel, sections, nz, ny), out_sha...]
where the time goes in v4:
time: 174 us
  Pallas kernels  169 us (97%)
  local copies, waits for them, and re-layouts  3.85 us (2%)
    pallas_call x1, Pallas kernels, per_device(): pl.pallas_call(functools.partial(relay_kernel, sections, nz, ny), out_sha...  169 us
    unnamed x2, local copies, waits for them, and re-layouts  3.85 us

profile of v4, /device:TPU:0, one launch (start us, length us, event | category | flops | bytes accessed | tf_op | source)
XLA Modules:
  0.0 173.9 jit_solution(18022544007523225014)
XLA Ops:
  1.3 168.7 %shard_map.86 = (bf16[1,128,4096]{2,1,0:T(8,128)(2,1)}, bf16[1,128,512]{2,1,0:T(8,128)(2,1)}) custom-call(s32[1]{0:T(128)S(6)} %copy.11.lost_ref, s32[4]{0:T(128)} %plan_ref.1, bf16[1,128,4096]{2,1,0:T(8,128)(2,1)} %pend_ref.1, bf16[4,128,512]{2,1,0:T(8,128)(2,1)} %pool_ref.1, bf16[3,4096,256]{2,1,0:T(8,128)(2,1)} %bitcast.4, bf16[256,4096]{1,0:T(8,128)(2,1)} %bitcast.5, ...), custom_call_target="tpu_custom_call" | custom-call | tf_op jit(solution)/shard_map/pallas_call | solution.py:312
  170.0 2.3 %copy.12 = bf16[1,128,4096]{2,1,0:T(8,128)(2,1)} copy(bf16[1,128,4096]{2,1,0:T(8,128)(2,1)} %get-tuple-element.4) | data formatting | bytes 2097152
  172.3 1.6 copy.13

commit v5 on v4

--- a/solution.py
+++ b/solution.py
@@ -11,7 +11,7 @@
 TICKS = 3
 NORM_EPS = 1e-05
 MESH = pl.DeviceIdType.MESH
-PIECES = 2
+PIECES = 4
 
 
 def relay_kernel(

time: 174 us -> 173 us (level)
  no operation moved by 1% of the time
where the time goes in v5:
time: 173 us
  Pallas kernels  168 us (97%)
  local copies, waits for them, and re-layouts  3.85 us (2%)
    pallas_call x1, Pallas kernels, per_device(): pl.pallas_call(functools.partial(relay_kernel, sections, nz, ny), out_sha...  168 us
    unnamed x2, local copies, waits for them, and re-layouts  3.85 us

profile of v5, /device:TPU:0, one launch (start us, length us, event | category | flops | bytes accessed | tf_op | source)
XLA Modules:
  0.0 172.9 jit_solution(5038142936994487237)
XLA Ops:
  1.3 167.8 %shard_map.86 = (bf16[1,128,4096]{2,1,0:T(8,128)(2,1)}, bf16[1,128,512]{2,1,0:T(8,128)(2,1)}) custom-call(s32[1]{0:T(128)S(6)} %copy.11.lost_ref, s32[4]{0:T(128)} %plan_ref.1, bf16[1,128,4096]{2,1,0:T(8,128)(2,1)} %pend_ref.1, bf16[4,128,512]{2,1,0:T(8,128)(2,1)} %pool_ref.1, bf16[3,4096,256]{2,1,0:T(8,128)(2,1)} %bitcast.4, bf16[256,4096]{1,0:T(8,128)(2,1)} %bitcast.5, ...), custom_call_target="tpu_custom_call" | custom-call | tf_op jit(solution)/shard_map/pallas_call | solution.py:312
  169.1 2.3 %copy.12 = bf16[1,128,4096]{2,1,0:T(8,128)(2,1)} copy(bf16[1,128,4096]{2,1,0:T(8,128)(2,1)} %get-tuple-element.4) | data formatting | bytes 2097152
  171.3 1.6 copy.13
